TPU v7x, 32 devices: a whole 2x2x4 slice. The times are simulated.
32 devices in a mesh: wide: 8 (over y, x, core), narrow: 4 (over z).
Axes of the slice: x: 2, y: 2, z: 4, core: 2. Of those that a mesh axis runs over, the one named last changes fastest.
Arguments:
- expression: bfloat16 [4000, 49152], P(None, ('wide', 'narrow')), may hold values from -60 to 60
- sketch_map: bfloat16 [64, 4000], replicated, may hold values from -0.09375 to 0.09375
Outputs:
- projected: float32 [64, 4000], P(None, 'narrow')
All inputs are finite; a program needn't handle non-finite values.
Results may differ from a plain program's by a relative error of at most 0.00037.
Values sent between devices are 32-bit elements; how exact they have to be, the bound alone decides.
A program may use at most 64 MiB of HBM per device.

v0:
```python
import functools

import jax
import jax.numpy as jnp
from jax import lax
from jax.experimental import pallas as pl
from jax.experimental.pallas import tpu as pltpu
from jax.sharding import PartitionSpec as P

LANES = 128
SUBLANES = 8
DEPTH = 512
PIECES = 4
LAG = 1
GRAM_AT = 1
EARLY = 40


def window_of(z, genes_own, width, padded):
    start = (z * genes_own) // LANES * LANES
    return jnp.minimum(start, padded - width)


def eliminate(blocks, first, last):
    row_id = lax.broadcasted_iota(jnp.int32, (SUBLANES, 1), 0)
    blocks = list(blocks)
    for k in range(first, last):
        home, r = divmod(k, SUBLANES)
        row = blocks[home][r : r + 1, :]
        scaled = row / row[:, k : k + 1]
        for i in range(home, len(blocks)):
            factor = blocks[i][:, k : k + 1]
            if i == home:
                factor = jnp.where(row_id > r, factor, 0.0)
            blocks[i] = blocks[i] - factor * scaled
    return blocks


def kernel(
    nw, nn, genes_own, width, padded, halvings,
    e_hbm, s_hbm, out_ref,
    e_ref, s_ref, skf, sk_ref, acc, gram, gat, zrecv, grecv, gzrecv, *rest,
):
    stages = max(nw.bit_length() - 1, 1)
    recvs = rest[:stages]
    (load_sem, st_send, st_recv, z_send, z_recv, ga_send, ga_recv, gr_send, gr_recv, gz_send, gz_recv) = rest[stages:]
    sketch, genes = s_ref.shape
    cells = e_ref.shape[1]
    w = lax.axis_index("wide")
    z = lax.axis_index("narrow")
    core = w % 2

    loads = [pltpu.make_async_copy(s_hbm, s_ref, load_sem.at[0])]
    cuts = list(range(0, genes, DEPTH)) + [genes]
    for b in range(len(cuts) - 1):
        rows = pl.ds(cuts[b], cuts[b + 1] - cuts[b])
        loads.append(pltpu.make_async_copy(e_hbm.at[rows], e_ref.at[rows], load_sem.at[b + 1]))
    for load in loads:
        load.start()

    def flip(power):
        return w + power - 2 * power * ((w // power) % 2)

    later = list(range(1, stages))
    turn = len(later) // 2
    other = later[turn:] + later[:turn]
    powers = [1] + [2**a + core * (2**b - 2**a) for a, b in zip(later, other)]
    peers = []
    for mask in range(1, 2 ** (halvings - 1)):
        peer = w
        for t in range(1, halvings):
            if mask >> (t - 1) & 1:
                peer = peer + powers[t] - 2 * powers[t] * ((w // powers[t]) % 2)
        peers.append((mask, peer))
    diagonal = [peer for mask, peer in peers if mask & (mask - 1)]

    barrier = pltpu.get_barrier_semaphore()
    for peer in diagonal:
        pl.semaphore_signal(barrier, inc=1, device_id={"wide": peer, "narrow": z})
    for t in range(stages):
        pl.semaphore_signal(barrier, inc=1, device_id={"wide": flip(2**t), "narrow": z})
    for d in range(1, nn):
        pl.semaphore_signal(barrier, inc=1, device_id={"wide": w, "narrow": (z + d) % nn})

    loads[0].wait()
    for b in range(len(cuts) - 1):
        loads[b + 1].wait()
        span = slice(cuts[b], cuts[b + 1])
        part = jnp.dot(s_ref[:, span], e_ref[span, :], preferred_element_type=jnp.float32)
        skf[...] = part if b == 0 else skf[...] + part
    sk = skf[...].astype(jnp.bfloat16)
    sk_ref[...] = sk
    total = lax.dot_general(sk, sk, (((1,), (1,)), ((), ())), preferred_element_type=jnp.float32)
    gram[...] = jnp.zeros_like(gram)
    gram[:, :sketch] = total
    pl.semaphore_wait(barrier, stages + nn - 1 + len(diagonal))

    bases, sizes = [], []
    base, size = 0, sketch
    for t in range(stages):
        if t < halvings:
            size //= 2
            bit = (w // powers[t]) % 2
            bases.append((pl.multiple_of(base + size * bit, SUBLANES), pl.multiple_of(base + size * (1 - bit), SUBLANES)))
            base = bases[-1][0]
        else:
            bases.append((base, base))
        sizes.append(size)

    def gram_copy(t):
        return pltpu.make_async_remote_copy(
            src_ref=gram, dst_ref=grecv.at[t], send_sem=gr_send.at[t], recv_sem=gr_recv.at[t],
            device_id={"wide": flip(2**t), "narrow": z},
        )

    def gram_z_copies():
        return [
            pltpu.make_async_remote_copy(
                src_ref=gram, dst_ref=gzrecv.at[d - 1], send_sem=gz_send.at[d - 1], recv_sem=gz_recv.at[d - 1],
                device_id={"wide": w, "narrow": (z + d) % nn},
            )
            for d in range(1, nn)
        ]

    chain = []

    def gram_next():
        t = len(chain)
        if t > stages:
            return
        if t > 0:
            chain[-1].wait()
            gram[...] = gram[...] + grecv[t - 1]
        if t < stages:
            copy = gram_copy(t)
            copy.start()
            chain.append(copy)
        else:
            copies = gram_z_copies()
            for copy in copies:
                copy.start()
            chain.append(copies)

    piece = padded // PIECES

    def stage_copy(t, p):
        lanes = pl.ds(p * piece, piece)
        return pltpu.make_async_remote_copy(
            src_ref=acc.at[pl.ds(bases[t][1], sizes[t]), lanes],
            dst_ref=recvs[t].at[:, lanes],
            send_sem=st_send.at[t, p], recv_sem=st_recv.at[t, p],
            device_id={"wide": flip(powers[t]), "narrow": z},
        )

    flying = {}

    def stage_start(t, p):
        flying[t, p] = stage_copy(t, p)
        flying[t, p].start()

    def stage_end(t, p):
        flying[t, p].wait()
        lanes = pl.ds(p * piece, piece)
        rows = pl.ds(bases[t][0], sizes[t])
        acc[rows, lanes] = acc[rows, lanes] + recvs[t][:, lanes]

    gram_next()
    if padded > genes:
        edge = genes // LANES * LANES
        acc[:, edge:] = jnp.zeros((sketch, padded - edge), jnp.float32)
    for p in range(PIECES):
        stop = min((p + 1) * piece, genes)
        acc[:, p * piece : stop] = lax.dot_general(
            sk_ref[...], e_ref[p * piece : stop, :], (((1,), (1,)), ((), ())),
            preferred_element_type=jnp.float32,
        )
        stage_start(0, p)
        if p == 1:
            gram_next()
        if p >= LAG:
            stage_end(0, p - LAG)
            if stages > 1:
                stage_start(1, p - LAG)
    gram_next()
    for p in range(PIECES - LAG, PIECES):
        stage_end(0, p)
        if stages > 1:
            stage_start(1, p)
    for t in range(1, stages):
        for p in range(PIECES):
            stage_end(t, p)
            if t + 1 < stages:
                stage_start(t + 1, p)
            if p == GRAM_AT:
                gram_next()

    own_rows = pl.ds(bases[-1][0], sizes[-1])
    z_copies = []
    for d in range(1, nn):
        to = (z + d) % nn
        start = pl.multiple_of(window_of(to, genes_own, width, padded), LANES)
        z_copies.append(
            pltpu.make_async_remote_copy(
                src_ref=acc.at[own_rows, pl.ds(start, width)], dst_ref=zrecv.at[d - 1],
                send_sem=z_send.at[d - 1], recv_sem=z_recv.at[d - 1],
                device_id={"wide": w, "narrow": to},
            )
        )
        z_copies[-1].start()
    while len(chain) <= stages:
        gram_next()
    for copy in chain[-1]:
        copy.wait()
    whole = gram[...]
    for d in range(1, nn):
        whole = whole + gzrecv[d - 1]
    lane = lax.broadcasted_iota(jnp.int32, (sketch, LANES), 1)
    line = lax.broadcasted_iota(jnp.int32, (sketch, LANES), 0)
    whole = jnp.where(lane == line + sketch, 1.0, whole)
    blocks = [whole[i : i + SUBLANES] for i in range(0, sketch, SUBLANES)]
    done = EARLY
    blocks = eliminate(blocks, 0, done)
    start = pl.multiple_of(window_of(z, genes_own, width, padded), LANES)
    mine = acc[own_rows, pl.ds(start, width)]
    for d in range(1, nn):
        z_copies[d - 1].wait()
        mine = mine + zrecv[d - 1]
    gat[own_rows, :] = mine
    def gather(rows, i, peer):
        return pltpu.make_async_remote_copy(
            src_ref=gat.at[rows], dst_ref=gat.at[rows],
            send_sem=ga_send.at[i], recv_sem=ga_recv.at[i],
            device_id={"wide": peer, "narrow": z},
        )

    copies = [gather(own_rows, mask, peer) for mask, peer in reversed(peers)]
    for copy in copies:
        copy.start()
    blocks = eliminate(blocks, done, sketch)
    reduced = jnp.concatenate(blocks, axis=0)
    pivots = jnp.sum(jnp.where(lane == line, reduced, 0.0), axis=1, keepdims=True)
    inverse = (reduced / jnp.sqrt(pivots))[:, sketch:]
    for copy in copies:
        copy.wait()
    copy = gather(pl.ds(bases[0][0], sizes[0]), 0, flip(1))
    copy.start()
    copy.wait()
    result = jnp.dot(
        inverse, gat[...], preferred_element_type=jnp.float32, precision=lax.Precision.HIGHEST
    )
    shift = z * genes_own - window_of(z, genes_own, width, padded)
    out_ref[...] = pltpu.roll(result, (width - shift) % width, 1)[:, :genes_own]


def solution(mesh):
    nw, nn = mesh.shape["wide"], mesh.shape["narrow"]

    def on_device(expression, sketch_map):
        genes, cells = expression.shape
        sketch = sketch_map.shape[0]
        genes_own = genes // nn
        padded = -(-genes // (LANES * PIECES)) * LANES * PIECES
        width = max(
            -(-(i + 1) * genes_own // LANES) - i * genes_own // LANES for i in range(nn)
        ) * LANES
        stages = nw.bit_length() - 1
        halvings = min(stages, (sketch // SUBLANES).bit_length() - 1)
        sizes = [max(sketch >> (t + 1), sketch >> halvings) for t in range(stages)]
        last = sizes[-1]
        dma = pltpu.SemaphoreType.DMA
        return pl.pallas_call(
            functools.partial(kernel, nw, nn, genes_own, width, padded, halvings),
            out_shape=jax.ShapeDtypeStruct((sketch, genes_own), jnp.float32),
            in_specs=[pl.BlockSpec(memory_space=pl.ANY)] * 2,
            out_specs=pl.BlockSpec(memory_space=pltpu.VMEM),
            scratch_shapes=[
                pltpu.VMEM((genes, cells), jnp.bfloat16),
                pltpu.VMEM((sketch, genes), jnp.bfloat16),
                pltpu.VMEM((sketch, cells), jnp.float32),
                pltpu.VMEM((sketch, cells), jnp.bfloat16),
                pltpu.VMEM((sketch, padded), jnp.float32),
                pltpu.VMEM((sketch, LANES), jnp.float32),
                pltpu.VMEM((sketch, width), jnp.float32),
                pltpu.VMEM((nn - 1, last, width), jnp.float32),
                pltpu.VMEM((stages, sketch, LANES), jnp.float32),
                pltpu.VMEM((nn - 1, sketch, LANES), jnp.float32),
            ]
            + [pltpu.VMEM((size, padded), jnp.float32) for size in sizes]
            + [
                dma((-(-genes // DEPTH) + 1,)),
                dma((stages, PIECES)),
                dma((stages, PIECES)),
                dma((nn - 1,)),
                dma((nn - 1,)),
                dma((2 ** (halvings - 1),)),
                dma((2 ** (halvings - 1),)),
                dma((stages,)),
                dma((stages,)),
                dma((nn - 1,)),
                dma((nn - 1,)),
            ],
            compiler_params=pltpu.CompilerParams(collective_id=0, has_side_effects=True),
        )(expression, sketch_map)

    placed = (P(None, ("wide", "narrow")), P())
    return jax.shard_map(
        on_device, mesh=mesh, in_specs=placed, out_specs=P(None, "narrow"), check_vma=False
    )
```

profile of v0, /device:TPU:0, one launch (start us, length us, event | category | flops | bytes accessed | tf_op | source)
XLA Modules:
  0.0 34.4 jit_solution(16575880933557410530)
XLA Ops:
  0.0 32.7 %shard_map.28 = f32[64,1000]{1,0:T(8,128)} custom-call(bf16[4000,1536]{1,0:T(8,128)(2,1)} %e_hbm.1, bf16[64,4000]{1,0:T(8,128)(2,1)} %s_hbm.1), custom_call_target="tpu_custom_call" | custom-call | tf_op jit(solution)/shard_map/pallas_call | solution.py:271
  32.7 1.7 %copy.4 = f32[64,1000]{1,0:T(8,128)} copy(f32[64,1000]{1,0:T(8,128)} %shard_map.28) | data formatting | bytes 512000
where the time goes:
time: 34.5 us; the launch traced here: 34.4 us
  Pallas kernels  32.7 us (95%)
  local copies, waits for them, and re-layouts  1.67 us (5%)
    pallas_call x1, Pallas kernels, on_device(): pl.pallas_call(functools.partial(kernel, nw, nn, genes_own, width, padded...  32.7 us
    unnamed x1, local copies, waits for them, and re-layouts  1.67 us

commit v1 on v0

--- a/solution.py
+++ b/solution.py
@@ -270,7 +270,7 @@
         dma = pltpu.SemaphoreType.DMA
         return pl.pallas_call(
             functools.partial(kernel, nw, nn, genes_own, width, padded, halvings),
-            out_shape=jax.ShapeDtypeStruct((sketch, genes_own), jnp.float32),
+            out_shape=pltpu.VMEM((sketch, genes_own), jnp.float32),
             in_specs=[pl.BlockSpec(memory_space=pl.ANY)] * 2,
             out_specs=pl.BlockSpec(memory_space=pltpu.VMEM),
             scratch_shapes=[

time: 34.5 us -> 32.9 us (0.954)
  local copies, waits for them, and re-layouts: 1.67 us -> 0.71 us
  Pallas kernels: 32.7 us -> 32 us
    unnamed x1, local copies, waits for them, and re-layouts: 1.67 us -> 0.71 us
    pallas_call x1, Pallas kernels: 32.7 us -> 32 us  [on_device(): pl.pallas_call(functools.partial(kernel, nw, nn, genes_own, width, padded...]
where the time goes in v1:
time: 32.9 us; the launch traced here: 32.7 us
  Pallas kernels  32 us (97%)
  local copies, waits for them, and re-layouts  0.71 us (2%)
    pallas_call x1, Pallas kernels, on_device(): pl.pallas_call(functools.partial(kernel, nw, nn, genes_own, width, padded...  32 us
    unnamed x1, local copies, waits for them, and re-layouts  0.71 us

profile of v1, /device:TPU:0, one launch (start us, length us, event | category | flops | bytes accessed | tf_op | source)
XLA Modules:
  0.0 32.7 jit_solution(11945157280098742111)
XLA Ops:
  0.0 32.0 %shard_map.28 = f32[64,1000]{1,0:T(8,128)S(1)} custom-call(bf16[4000,1536]{1,0:T(8,128)(2,1)} %e_hbm.1, bf16[64,4000]{1,0:T(8,128)(2,1)} %s_hbm.1), custom_call_target="tpu_custom_call" | custom-call | tf_op jit(solution)/shard_map/pallas_call | solution.py:271
  32.0 0.7 %copy.4 = f32[64,1000]{1,0:T(8,128)} copy(f32[64,1000]{1,0:T(8,128)S(1)} %shard_map.28) | data formatting | bytes 512000
